TPU v7x, 32 devices: a whole 2x2x4 slice. The times are simulated.
32 devices in a mesh: dp: 8 (over y, x, core), expert: 4 (over z).
Axes of the slice: x: 2, y: 2, z: 4, core: 2. Of those that a mesh axis runs over, the one named last changes fastest.
Arguments:
- grad_out: bfloat16 [20480, 1024], P(('dp', 'expert')), may hold values from -3 to 3
- hidden_acts: bfloat16 [20480, 384], P(('dp', 'expert')), may hold values from -0.23925781 to 0.23925781
- expert_ids: int32 [20480], P(('dp', 'expert')), may hold values from 0 to 3, as said below
- down_weight: bfloat16 [4, 384, 1024], P('expert'), may hold values from -0.1875 to 0.1875
- error_in: bfloat16 [8, 4, 384, 1024], P('dp', 'expert'), may hold values from -0.8984375 to 0.8984375
- q_prev: float32 [4, 1024, 32], P('expert'), may hold values from -6 to 6
Outputs:
- grad_hidden: bfloat16 [20480, 384], P(('dp', 'expert'))
- left_factor: float32 [4, 384, 32], P('expert')
- right_factor: float32 [4, 1024, 32], P('expert')
- error_out: bfloat16 [8, 4, 384, 1024], P('dp', 'expert')
Inputs may be any that keep to these rules, and one draw needn't show every extreme that they name: `expert_ids`: the rows of one device name each expert at most 320 times; in every replica some expert is named exactly 320 times by the rows of every device of that replica.
All inputs are finite; a program needn't handle non-finite values.
Results may differ from a plain program's by a relative error of at most 0.0004.
Values may be sent and summed in bfloat16 or wider, within the bound.
No kernel may reach another device: no remote copies, remote signals or barrier semaphores. Data moves between devices by JAX's collectives and lax.ppermute only.
A program may use at most 64 MiB of HBM per device.

v0:
```python
import jax
import jax.numpy as jnp
from jax import lax
from jax.sharding import PartitionSpec as P


def place_rows(expert_list, count):
    onehot = (expert_list[:, None] == jnp.arange(count, dtype=jnp.int32)[None, :]).astype(jnp.int32)
    ranks = jnp.cumsum(onehot, axis=0) - 1
    return jnp.sum(ranks * onehot, axis=1)


def orthonormal(block, gram):
    chol = jnp.linalg.cholesky(gram)
    return lax.linalg.triangular_solve(chol, block, left_side=False, lower=True, transpose_a=True)


def shards(grad_out, hidden_acts, expert_ids, down_weight, error_in, q_prev):
    experts = lax.axis_size("expert")
    row_count = grad_out.shape[0]
    capacity = 2 * row_count // experts
    width = grad_out.shape[1]
    hidden_width = hidden_acts.shape[1]
    position = place_rows(expert_ids, experts)
    slot_index = expert_ids * capacity + position
    grad_buffer = jnp.zeros((experts * capacity, width), jnp.bfloat16).at[slot_index].set(grad_out)
    grad_buffer = grad_buffer.reshape(experts, capacity, width)
    hidden_buffer = (
        jnp.zeros((experts * capacity, hidden_width), jnp.bfloat16).at[slot_index].set(hidden_acts)
    )
    hidden_buffer = hidden_buffer.reshape(experts, capacity, hidden_width)
    weight = down_weight[0]
    grad_recv, hidden_recv = (
        lax.all_to_all(grad_buffer, "expert", split_axis=0, concat_axis=0, tiled=True),
        lax.all_to_all(hidden_buffer, "expert", split_axis=0, concat_axis=0, tiled=True),
    )
    product = lax.dot_general(
        grad_recv, weight, (((2,), (1,)), ((), ())), preferred_element_type=jnp.float32
    )
    back = lax.all_to_all(
        product.astype(jnp.bfloat16), "expert", split_axis=0, concat_axis=0, tiled=True
    )
    grads = lax.dot_general(
        hidden_recv.reshape(-1, hidden_width),
        grad_recv.reshape(-1, width),
        (((0,), (0,)), ((), ())),
        preferred_element_type=jnp.float32,
    )
    grad_hidden = back.reshape(experts * capacity, hidden_width)[slot_index]
    merged = grads + error_in[0, 0].astype(jnp.float32)
    highest = lax.Precision.HIGHEST
    left_local = jnp.dot(merged, q_prev[0], precision=highest)
    left_sum = lax.psum(left_local, "dp")
    gram = jnp.dot(left_sum.T, left_sum, precision=highest)
    left_factor = orthonormal(left_sum, gram)
    right_local = lax.dot_general(merged, left_factor, (((0,), (0,)), ((), ())), precision=highest)
    right_factor = lax.psum(right_local, "dp") / lax.axis_size("dp")
    approx = jnp.dot(left_factor, right_factor.T, precision=highest)
    error_out = (merged - approx).astype(jnp.bfloat16)
    return (grad_hidden, left_factor[None], right_factor[None], error_out[None, None])


def solution(mesh):
    placed = (
        P(("dp", "expert"), None),
        P(("dp", "expert"), None),
        P(("dp", "expert")),
        P("expert", None, None),
        P("dp", "expert", None, None),
        P("expert", None, None),
    )
    return jax.shard_map(
        shards,
        mesh=mesh,
        in_specs=placed,
        out_specs=(
            P(("dp", "expert"), None),
            P("expert", None, None),
            P("expert", None, None),
            P("dp", "expert", None, None),
        ),
        check_vma=False,
    )
```

profile of v0, /device:TPU:0, one launch (start us, length us, event | category | flops | bytes accessed | tf_op | source)
XLA Modules:
  0.0 222.1 jit_solution(1954944167356880882)
XLA Ops:
  7.2 0.0 copy-start
  7.2 0.8 fusion.14
  7.9 1.1 reduce-window.6
  9.1 0.2 slice_reduce_fusion
  9.3 0.2 reduce-window.9
  9.5 0.1 add_bitcast_fusion
  9.5 0.7 fusion.16
  10.3 0.7 compare_select_fusion
  11.0 7.1 %scatter_custom_fusion.1 = bf16[1280,384]{1,0:T(8,128)(2,1)} fusion(s32[640]{0:T(1024)S(1)} %compare_select_fusion, bf16[640,384]{1,0:T(8,128)(2,1)} %param.7, bf16[]{:T(256)} %constant.51.clone.1), kind=kCustom, calls=%fused_computation.10 | custom fusion | bytes 983552 | tf_op jit(solution)/shard_map/scatter | solution.py:29
  18.1 6.3 %all-to-all-start.2 = ((bf16[4,320,384]{2,1,0:T(8,128)(2,1)}), bf16[4,320,384]{2,1,0:T(8,128)(2,1)S(1)}, u32[]{:S(2)}, u32[]{:S(2)}) async-start(bf16[4,320,384]{2,1,0:T(8,128)(2,1)} %bitcast.6), calls=%async_computation.2 | async-start | bytes 1966080 | tf_op jit(solution)/shard_map/all_to_all | solution.py:35
  24.4 8.2 %scatter_custom_fusion = bf16[1280,1024]{1,0:T(8,128)(2,1)} fusion(s32[640]{0:T(1024)S(1)} %compare_select_fusion, bf16[640,1024]{1,0:T(8,128)(2,1)} %param.6, bf16[]{:T(256)} %constant.51.clone.1), kind=kCustom, calls=%fused_computation.6 | custom fusion | bytes 2621952 | tf_op jit(solution)/shard_map/scatter | solution.py:26
  32.6 16.1 %all-to-all-done.2 = bf16[4,320,384]{2,1,0:T(8,128)(2,1)S(1)} async-done(((bf16[4,320,384]{2,1,0:T(8,128)(2,1)}), bf16[4,320,384]{2,1,0:T(8,128)(2,1)S(1)}, u32[]{:S(2)}, u32[]{:S(2)}) %all-to-all-start.2) | async-done | bytes 983072 | tf_op jit(solution)/shard_map/all_to_all | solution.py:35
  48.7 0.0 copy-start.2
  48.7 62.7 %all_to_all.15 = bf16[4,320,1024]{2,1,0:T(8,128)(2,1)S(1)} all-to-all(bf16[4,320,1024]{2,1,0:T(8,128)(2,1)} %bitcast.56), channel_id=1, replica_groups=mesh['dp'=8,'expert'=4] {'expert'}, dimensions={0} | all-to-all | bytes 5242880 | tf_op jit(solution)/shard_map/all_to_all | solution.py:34
  111.5 0.0 copy-done.2
  111.5 0.0 copy-start.1
  111.5 0.0 copy-start.5
  111.5 1.2 convert_add_fusion
  112.7 0.3 copy-done.1
  113.0 0.0 copy-done.5
  113.0 1.5 fusion.6
  114.5 23.2 %psum.14 = f32[384,32]{0,1:T(8,128)S(1)} all-reduce(f32[384,32]{0,1:T(8,128)S(1)} %fusion.6), channel_id=1, replica_groups=mesh['dp'=8,'expert'=4] {'dp'}, use_global_device_ids=true, to_apply=%region_5.6 | all-reduce | flops 12288 | bytes 98304 | tf_op jit(solution)/shard_map/psum | solution.py:53
  137.7 0.2 fusion.18
  137.9 0.1 copy.11
  138.0 0.0 copy-done
  138.0 4.3 %convolution_convert_fusion = bf16[4,320,384]{2,1,0:T(8,128)(2,1)} fusion(bf16[4,320,1024]{2,1,0:T(8,128)(2,1)} %copy-done.1, bf16[1,384,1024]{2,1,0:T(8,128)(2,1)S(1)} %copy-done), kind=kOutput, calls=%fused_computation.5 | convolution fusion | flops 1007124480 | bytes 4390912 | tf_op jit(solution)/shard_map/dot_general | solution.py:37
  142.3 3.6 %all-to-all-start.1 = ((bf16[4,320,384]{2,1,0:T(8,128)(2,1)}), bf16[4,320,384]{2,1,0:T(8,128)(2,1)S(1)}, u32[]{:S(2)}, u32[]{:S(2)}) async-start(bf16[4,320,384]{2,1,0:T(8,128)(2,1)} %convolution_convert_fusion), calls=%async_computation.1 | async-start | bytes 1966080 | tf_op jit(solution)/shard_map/all_to_all | solution.py:40
  145.8 0.2 all-reduce.2.cloned.1.call-start
  146.0 2.9 %cholesky.16 = f32[32,32]{1,0:T(8,128)S(1)} custom-call(f32[32,32]{1,0:T(8,128)S(1)} %fusion.13), custom_call_target="Cholesky" | custom-call | tf_op jit(solution)/shard_map/jit(cholesky)/cholesky | solution.py:14
  149.0 0.6 compare_reduce_fusion
  149.6 0.7 fusion.10
  150.3 2.5 %custom-call.6 = f32[1,32,32]{1,2,0:T(8,128)S(1)} custom-call(f32[1,32,32]{2,1,0:T(8,128)S(1)} %fusion.10), custom_call_target="InvertDiagBlocksLowerTriangular" | custom-call | tf_op jit(solution)/shard_map/triangular_solve | solution.py:15
  152.7 0.2 fusion.11
  153.0 0.0 copy-start.4
  153.0 1.7 fusion.19
  154.7 0.0 all-reduce.2.cloned.1.call-update
  154.7 53.3 %all-reduce.2.cloned.1.call-done = f32[1024,32]{0,1:T(8,128)} async-done(((f32[1024,32]{0,1:T(8,128)}), f32[1024,32]{0,1:T(8,128)}) %all-reduce.2.cloned.1.call-update) | async-done | bytes 131088 | tf_op jit(solution)/shard_map/psum | solution.py:57
  208.1 0.0 copy-start.3
  208.1 3.3 %fusion.2 = bf16[1,1,384,1024]{3,2,1,0:T(8,128)(2,1)} fusion(f32[384,1024]{1,0:T(8,128)S(1)} %convert_add_fusion, f32[384,32]{0,1:T(8,128)S(1)} %fusion.11, f32[1024,32]{0,1:T(8,128)} %all-reduce.2.cloned.1.call-done), kind=kOutput, calls=%fused_computation.8 | convolution fusion | flops 151814144 | bytes 2539520 | tf_op jit(solution)/shard_map/dot_general | solution.py:58
  211.4 0.0 copy-done.4
  211.4 0.0 copy-done.3
  211.4 0.7 multiply_bitcast_fusion
  212.0 0.0 all-to-all-done.1
  212.0 3.2 %gather_fusion = bf16[640,384]{1,0:T(8,128)(2,1)} fusion(bf16[1280,384]{1,0:T(8,128)(2,1)S(1)} %bitcast.55, s32[1024]{0:T(1024)S(1)} %pad_clamp_fusion), kind=kCustom, calls=%fused_computation | custom fusion | bytes 985600 | tf_op jit(solution)/shard_map/gather | solution.py:49
  (3 shorter events, 0.0 us)
Async XLA Ops:
  7.2 130.8 %copy-start = (bf16[1,384,1024]{2,1,0:T(8,128)(2,1)S(1)}, bf16[1,384,1024]{2,1,0:T(8,128)(2,1)}, u32[]{:S(2)}) copy-start(bf16[1,384,1024]{2,1,0:T(8,128)(2,1)} %param.9) | copy-start | bytes 2359300
  18.1 30.7 %all-to-all-start.2 = ((bf16[4,320,384]{2,1,0:T(8,128)(2,1)}), bf16[4,320,384]{2,1,0:T(8,128)(2,1)S(1)}, u32[]{:S(2)}, u32[]{:S(2)}) async-start(bf16[4,320,384]{2,1,0:T(8,128)(2,1)} %bitcast.6), calls=%async_computation.2 | async-start | bytes 1966080 | tf_op jit(solution)/shard_map/all_to_all | solution.py:35
  48.7 62.8 %copy-start.2 = (bf16[1,1,384,1024]{3,2,1,0:T(8,128)(2,1)S(1)}, bf16[1,1,384,1024]{3,2,1,0:T(8,128)(2,1)}, u32[]{:S(2)}) copy-start(bf16[1,1,384,1024]{3,2,1,0:T(8,128)(2,1)} %param.10) | copy-start | bytes 2359300
  111.5 1.5 copy-start.1
  111.5 1.5 copy-start.5
  142.3 69.8 %all-to-all-start.1 = ((bf16[4,320,384]{2,1,0:T(8,128)(2,1)}), bf16[4,320,384]{2,1,0:T(8,128)(2,1)S(1)}, u32[]{:S(2)}, u32[]{:S(2)}) async-start(bf16[4,320,384]{2,1,0:T(8,128)(2,1)} %convolution_convert_fusion), calls=%async_computation.1 | async-start | bytes 1966080 | tf_op jit(solution)/shard_map/all_to_all | solution.py:40
  145.8 62.2 %all-reduce.2.cloned.1.call-start = ((), (), s32[]{:S(2)}) async-start(), calls=%async_computation.3 | async-start | bytes 262144 | tf_op jit(solution)/shard_map/psum | solution.py:57
  153.0 58.4 %copy-start.4 = (f32[384,32]{0,1:T(8,128)}, f32[384,32]{0,1:T(8,128)S(1)}, u32[]{:S(2)}) copy-start(f32[384,32]{0,1:T(8,128)S(1)} %fusion.11) | copy-start | bytes 147460
  208.1 3.3 %copy-start.3 = (f32[1024,32]{0,1:T(8,128)S(1)}, f32[1024,32]{0,1:T(8,128)}, u32[]{:S(2)}) copy-start(f32[1024,32]{0,1:T(8,128)} %all-reduce.2.cloned.1.call-done) | copy-start | bytes 393220
Sparse Core Ops, SparseCore 0:
  154.8 53.1 all-reduce.1
where the time goes:
time: 223 us; the launch traced here: 222 us
  blocking collectives  86 us (39%)
  waiting for transfers between devices  69.4 us (31%)
  local copies, waits for them, and re-layouts  19.1 us (9%)
  between operations  14.1 us (6%)
  matrix products  12.4 us (6%)
  other arithmetic  10.9 us (5%)
  starting transfers between devices  10.1 us (5%)
    all_to_all x1, blocking collectives, shards(): lax.all_to_all(grad_buffer, 'expert', split_axis=0, concat_axis=0, tiled=...  62.7 us
    psum x1, waiting for transfers between devices, shards(): right_factor = lax.psum(right_local, 'dp') / lax.axis_size('dp')  53.3 us
    psum x1, blocking collectives, shards(): left_sum = lax.psum(left_local, 'dp')  23.2 us
    all_to_all x1, waiting for transfers between devices, shards(): lax.all_to_all(hidden_buffer, 'expert', split_axis=0, concat_axis=0, tile...  16.1 us
    scatter x1, local copies, waits for them, and re-layouts, shards(): jnp.zeros((experts * capacity, width), jnp.bfloat16).at[slot_index]  8.24 us
    scatter x1, local copies, waits for them, and re-layouts, shards(): jnp.zeros((experts * capacity, hidden_width), jnp.bfloat16).at[slot_index]  7.1 us
    all_to_all x1, starting transfers between devices, shards(): lax.all_to_all(hidden_buffer, 'expert', split_axis=0, concat_axis=0, tile...  6.35 us
  transfers between devices with their start and end apart: 3, of which 2 were waited for; matrix products, arithmetic and copies ran while one was open for 9% of the time, Pallas kernels for 0%

commit v1 on v0

--- a/solution.py
+++ b/solution.py
@@ -2,6 +2,11 @@
 import jax.numpy as jnp
 from jax import lax
 from jax.sharding import PartitionSpec as P
+
+
+def gather_and_add(x, name):
+    parts = lax.all_gather(x, name)
+    return jnp.sum(parts, axis=0)
 
 
 def place_rows(expert_list, count):
@@ -54,7 +59,7 @@
     gram = jnp.dot(left_sum.T, left_sum, precision=highest)
     left_factor = orthonormal(left_sum, gram)
     right_local = lax.dot_general(merged, left_factor, (((0,), (0,)), ((), ())), precision=highest)
-    right_factor = lax.psum(right_local, "dp") / lax.axis_size("dp")
+    right_factor = gather_and_add(right_local, "dp") / lax.axis_size("dp")
     approx = jnp.dot(left_factor, right_factor.T, precision=highest)
     error_out = (merged - approx).astype(jnp.bfloat16)
     return (grad_hidden, left_factor[None], right_factor[None], error_out[None, None])

time: 223 us -> 192 us (0.86)
  waiting for transfers between devices: 69.4 us -> 38.2 us
    psum x1 -> x0, waiting for transfers between devices: 53.3 us -> none  [shards(): right_factor = lax.psum(right_local, 'dp') / lax.axis_size('dp')]
    all_to_all x1, waiting for transfers between devices: 0.01 us -> 22.1 us  [shards(): lax.all_to_all(product.astype(jnp.bfloat16), 'expert', split_axis=0, conc...]
  transfers between devices with their start and end apart: 3 -> 3, of which waited for: 2 -> 2; matrix products, arithmetic and copies ran while one was open for 9% -> 8% of each run, Pallas kernels for 0% -> 0%
where the time goes in v1:
time: 192 us
  blocking collectives  86 us (45%)
  waiting for transfers between devices  38.2 us (20%)
  local copies, waits for them, and re-layouts  21 us (11%)
  between operations  14.1 us (7%)
  matrix products  11.4 us (6%)
  other arithmetic  11.2 us (6%)
  starting transfers between devices  9.92 us (5%)
    all_to_all x1, blocking collectives, shards(): lax.all_to_all(grad_buffer, 'expert', split_axis=0, concat_axis=0, tiled=...  62.7 us
    psum x1, blocking collectives, shards(): left_sum = lax.psum(left_local, 'dp')  23.2 us
    all_to_all x1, waiting for transfers between devices, shards(): lax.all_to_all(product.astype(jnp.bfloat16), 'expert', split_axis=0, conc...  22.1 us
    all_to_all x1, waiting for transfers between devices, shards(): lax.all_to_all(hidden_buffer, 'expert', split_axis=0, concat_axis=0, tile...  16.1 us
    scatter x1, local copies, waits for them, and re-layouts, shards(): jnp.zeros((experts * capacity, width), jnp.bfloat16).at[slot_index]  8.24 us
    scatter x1, local copies, waits for them, and re-layouts, shards(): jnp.zeros((experts * capacity, hidden_width), jnp.bfloat16).at[slot_index]  7.1 us
    all_to_all x1, starting transfers between devices, shards(): lax.all_to_all(hidden_buffer, 'expert', split_axis=0, concat_axis=0, tile...  6.35 us
    dot_general x1, matrix products, shards(): lax.dot_general(grad_recv, weight, (((2,), (1,)), ((), ())), preferred_el...  4.22 us
  transfers between devices with their start and end apart: 3, of which 2 were waited for; matrix products, arithmetic and copies ran while one was open for 8% of the time, Pallas kernels for 0%

profile of v1, /device:TPU:0, one launch (start us, length us, event | category | flops | bytes accessed | tf_op | source)
XLA Modules:
  0.0 191.8 jit_solution(1631044556661522230)
XLA Ops:
  7.2 0.0 copy-start
  7.2 0.8 fusion.14
  7.9 1.1 reduce-window.6
  9.1 0.2 slice_reduce_fusion
  9.3 0.2 reduce-window.9
  9.5 0.1 add_bitcast_fusion
  9.5 0.7 fusion.16
  10.3 0.7 compare_select_fusion
  11.0 7.1 %scatter_custom_fusion.1 = bf16[1280,384]{1,0:T(8,128)(2,1)} fusion(s32[640]{0:T(1024)S(1)} %compare_select_fusion, bf16[640,384]{1,0:T(8,128)(2,1)} %param.7, bf16[]{:T(256)} %constant.52.clone.1), kind=kCustom, calls=%fused_computation.11 | custom fusion | bytes 983552 | tf_op jit(solution)/shard_map/scatter | solution.py:34
  18.1 6.3 %all-to-all-start.2 = ((bf16[4,320,384]{2,1,0:T(8,128)(2,1)}), bf16[4,320,384]{2,1,0:T(8,128)(2,1)S(1)}, u32[]{:S(2)}, u32[]{:S(2)}) async-start(bf16[4,320,384]{2,1,0:T(8,128)(2,1)} %bitcast.6), calls=%async_computation.2 | async-start | bytes 1966080 | tf_op jit(solution)/shard_map/all_to_all | solution.py:40
  24.4 0.0 all-gather.3.cloned.1.call-start
  24.4 8.2 %scatter_custom_fusion = bf16[1280,1024]{1,0:T(8,128)(2,1)} fusion(s32[640]{0:T(1024)S(1)} %compare_select_fusion, bf16[640,1024]{1,0:T(8,128)(2,1)} %param.6, bf16[]{:T(256)} %constant.52.clone.1), kind=kCustom, calls=%fused_computation.6 | custom fusion | bytes 2621952 | tf_op jit(solution)/shard_map/scatter | solution.py:31
  32.6 16.1 %all-to-all-done.2 = bf16[4,320,384]{2,1,0:T(8,128)(2,1)S(1)} async-done(((bf16[4,320,384]{2,1,0:T(8,128)(2,1)}), bf16[4,320,384]{2,1,0:T(8,128)(2,1)S(1)}, u32[]{:S(2)}, u32[]{:S(2)}) %all-to-all-start.2) | async-done | bytes 983072 | tf_op jit(solution)/shard_map/all_to_all | solution.py:40
  48.7 0.0 copy-start.2
  48.7 62.7 %all_to_all.15 = bf16[4,320,1024]{2,1,0:T(8,128)(2,1)S(1)} all-to-all(bf16[4,320,1024]{2,1,0:T(8,128)(2,1)} %bitcast.61), channel_id=1, replica_groups=mesh['dp'=8,'expert'=4] {'expert'}, dimensions={0} | all-to-all | bytes 5242880 | tf_op jit(solution)/shard_map/all_to_all | solution.py:39
  111.5 0.0 copy-done.2
  111.5 0.0 copy-start.1
  111.5 0.0 copy-start.4
  111.5 1.2 convert_add_fusion
  112.7 0.3 copy-done.1
  113.0 0.0 copy-done.4
  113.0 1.5 fusion.6
  114.5 23.2 %psum.7 = f32[384,32]{0,1:T(8,128)S(1)} all-reduce(f32[384,32]{0,1:T(8,128)S(1)} %fusion.6), channel_id=1, replica_groups=mesh['dp'=8,'expert'=4] {'dp'}, use_global_device_ids=true, to_apply=%region_5.6 | all-reduce | flops 12288 | bytes 98304 | tf_op jit(solution)/shard_map/psum | solution.py:58
  137.7 0.2 fusion.18
  137.9 0.1 copy.11
  138.0 2.9 %cholesky.16 = f32[32,32]{1,0:T(8,128)S(1)} custom-call(f32[32,32]{1,0:T(8,128)S(1)} %fusion.13), custom_call_target="Cholesky" | custom-call | tf_op jit(solution)/shard_map/jit(cholesky)/cholesky | solution.py:19
  141.0 0.6 compare_reduce_fusion
  141.6 0.7 fusion.10
  142.3 2.4 %custom-call.6 = f32[1,32,32]{1,2,0:T(8,128)S(1)} custom-call(f32[1,32,32]{2,1,0:T(8,128)S(1)} %fusion.10), custom_call_target="InvertDiagBlocksLowerTriangular" | custom-call | tf_op jit(solution)/shard_map/triangular_solve | solution.py:20
  144.7 0.3 fusion.11
  145.0 0.0 copy-start.3
  145.0 1.7 fusion.19
  146.7 0.0 all-gather.3.cloned.1.call-update
  146.7 0.0 copy-done
  146.7 4.2 %convolution_convert_fusion = bf16[4,320,384]{2,1,0:T(8,128)(2,1)} fusion(bf16[4,320,1024]{2,1,0:T(8,128)(2,1)} %copy-done.1, bf16[1,384,1024]{2,1,0:T(8,128)(2,1)S(1)} %copy-done), kind=kOutput, calls=%fused_computation.5 | convolution fusion | flops 1007124480 | bytes 4390912 | tf_op jit(solution)/shard_map/dot_general | solution.py:42
  150.9 3.6 %all-to-all-start.1 = ((bf16[4,320,384]{2,1,0:T(8,128)(2,1)}), bf16[4,320,384]{2,1,0:T(8,128)(2,1)S(1)}, u32[]{:S(2)}, u32[]{:S(2)}) async-start(bf16[4,320,384]{2,1,0:T(8,128)(2,1)} %convolution_convert_fusion), calls=%async_computation.1 | async-start | bytes 1966080 | tf_op jit(solution)/shard_map/all_to_all | solution.py:45
  154.5 22.1 %all-to-all-done.1 = bf16[4,320,384]{2,1,0:T(8,128)(2,1)S(1)} async-done(((bf16[4,320,384]{2,1,0:T(8,128)(2,1)}), bf16[4,320,384]{2,1,0:T(8,128)(2,1)S(1)}, u32[]{:S(2)}, u32[]{:S(2)}) %all-to-all-start.1) | async-done | bytes 983072 | tf_op jit(solution)/shard_map/all_to_all | solution.py:45
  176.6 3.2 %gather_fusion = bf16[640,384]{1,0:T(8,128)(2,1)} fusion(bf16[1280,384]{1,0:T(8,128)(2,1)S(1)} %bitcast.60, s32[1024]{0:T(1024)S(1)} %pad_clamp_fusion), kind=kCustom, calls=%fused_computation | custom fusion | bytes 985600 | tf_op jit(solution)/shard_map/gather | solution.py:54
  179.8 0.0 all-gather.3.cloned.1.call-done
  179.8 1.8 copy.13
  181.7 0.3 bitcast_reduce_fusion
  181.9 0.7 multiply_bitcast_fusion
  182.6 0.0 copy-done.3
  182.6 2.3 %fusion.2 = bf16[1,1,384,1024]{3,2,1,0:T(8,128)(2,1)} fusion(f32[384,1024]{1,0:T(8,128)S(1)} %convert_add_fusion, f32[384,32]{0,1:T(8,128)S(1)} %fusion.11, f32[1024,32]{0,1:T(8,128)S(1)} %bitcast_reduce_fusion), kind=kOutput, calls=%fused_computation.8 | convolution fusion | flops 151814144 | bytes 2539520 | tf_op jit(solution)/shard_map/dot_general | solution.py:63
  (3 shorter events, 0.0 us)
Async XLA Ops:
  7.2 139.5 %copy-start = (bf16[1,384,1024]{2,1,0:T(8,128)(2,1)S(1)}, bf16[1,384,1024]{2,1,0:T(8,128)(2,1)}, u32[]{:S(2)}) copy-start(bf16[1,384,1024]{2,1,0:T(8,128)(2,1)} %param.9) | copy-start | bytes 2359300
  18.1 30.7 %all-to-all-start.2 = ((bf16[4,320,384]{2,1,0:T(8,128)(2,1)}), bf16[4,320,384]{2,1,0:T(8,128)(2,1)S(1)}, u32[]{:S(2)}, u32[]{:S(2)}) async-start(bf16[4,320,384]{2,1,0:T(8,128)(2,1)} %bitcast.6), calls=%async_computation.2 | async-start | bytes 1966080 | tf_op jit(solution)/shard_map/all_to_all | solution.py:40
  24.4 155.4 %all-gather.3.cloned.1.call-start = ((), (), s32[]{:S(2)}) async-start(), calls=%async_computation.3 | async-start | bytes 1179648 | tf_op jit(solution)/shard_map/all_gather | solution.py:8
  48.7 62.8 %copy-start.2 = (bf16[1,1,384,1024]{3,2,1,0:T(8,128)(2,1)S(1)}, bf16[1,1,384,1024]{3,2,1,0:T(8,128)(2,1)}, u32[]{:S(2)}) copy-start(bf16[1,1,384,1024]{3,2,1,0:T(8,128)(2,1)} %param.10) | copy-start | bytes 2359300
  111.5 1.5 copy-start.1
  111.5 1.5 copy-start.4
  145.0 37.6 %copy-start.3 = (f32[384,32]{0,1:T(8,128)}, f32[384,32]{0,1:T(8,128)S(1)}, u32[]{:S(2)}) copy-start(f32[384,32]{0,1:T(8,128)S(1)} %fusion.11) | copy-start | bytes 147460
  150.9 25.7 %all-to-all-start.1 = ((bf16[4,320,384]{2,1,0:T(8,128)(2,1)}), bf16[4,320,384]{2,1,0:T(8,128)(2,1)S(1)}, u32[]{:S(2)}, u32[]{:S(2)}) async-start(bf16[4,320,384]{2,1,0:T(8,128)(2,1)} %convolution_convert_fusion), calls=%async_computation.1 | async-start | bytes 1966080 | tf_op jit(solution)/shard_map/all_to_all | solution.py:45
Sparse Core Ops, SparseCore 0:
  146.8 21.4 all-gather.2
